TPU v7x, 32 devices: a 4x4x1 block of a 4x4x8 slice. The times are simulated.
32 devices in a mesh: dp: 1 (over z), tp: 32 (over x, y, core).
Axes of the slice: x: 4, y: 4, z: 1, core: 2. Of those that a mesh axis runs over, the one named last changes fastest.
The devices are a block of a 4x4x8 slice.
Arguments:
- x: bfloat16 [7168, 5120], P(('dp', 'tp'))
- dy: bfloat16 [7168, 5120], P(('dp', 'tp'))
- gate: bfloat16 [7168, 12288], P('dp', 'tp')
- up: bfloat16 [7168, 12288], P('dp', 'tp')
- w_gate: bfloat16 [5120, 12288], P(None, 'tp')
- w_up: bfloat16 [5120, 12288], P(None, 'tp')
- w_down: bfloat16 [12288, 5120], P('tp')
Outputs:
- output 1: bfloat16 [7168, 5120], P(('dp', 'tp'))
- output 2: bfloat16 [5120, 12288], P('dp', 'tp')
- output 3: bfloat16 [5120, 12288], P('dp', 'tp')
- output 4: bfloat16 [12288, 5120], P(('dp', 'tp'))
All inputs are finite; a program needn't handle non-finite values.
Results may differ from a plain program's by a relative error of at most 0.012.
Values are sent between devices in bfloat16 or wider.
A program may use at most 768 MiB of HBM per device.

v0:
```python
import jax
import jax.numpy as jnp


def act(gate, up):
    return jax.nn.silu(gate) * up


def solution(mesh):
    def step(x, dy, gate, up, w_gate, w_up, w_down):
        hidden, back = jax.vjp(act, gate.astype(jnp.float32), up.astype(jnp.float32))
        d_hidden = jnp.dot(dy, w_down.T, preferred_element_type=jnp.float32)
        d_gate, d_up = (g.astype(jnp.bfloat16) for g in back(d_hidden))
        dx = jnp.dot(d_gate, w_gate.T) + jnp.dot(d_up, w_up.T)
        groups = mesh.shape["dp"]

        def by_group(a, b):
            a, b = (t.reshape(groups, -1, t.shape[-1]) for t in (a, b))
            product = jnp.einsum("gta,gtb->gab", a, b, preferred_element_type=jnp.float32)
            return product.astype(jnp.bfloat16).reshape(-1, b.shape[-1])

        return dx, by_group(x, d_gate), by_group(x, d_up), by_group(hidden.astype(jnp.bfloat16), dy)

    return step
```

profile of v0, /device:TPU:97, one launch (start us, length us, event | category | flops | bytes accessed | tf_op | source)
XLA Modules:
  0.0 753.3 jit_solution(9893026279038532454)
XLA Ops:
  7.2 0.1 all-gather.7.cloned.1.call-start
  7.2 0.7 all-gather.7.cloned.1.call-update
  8.0 0.1 all-gather.9.cloned.1.call-start
  8.0 0.7 all-gather.9.cloned.1.call-update
  8.8 0.1 reduce-scatter.5.cloned.1.call-start
  8.9 217.8 %all-gather.7.cloned.1.call-done = bf16[7168,5120]{1,0:T(8,128)(2,1)} async-done(((bf16[224,5120]{1,0:T(8,128)(2,1)}), bf16[7168,5120]{1,0:T(8,128)(2,1)}) %all-gather.7.cloned.1.call-update) | async-done | bytes 73400336 | tf_op args[1]
  226.6 51.4 %fusion.6 = (bf16[7168,384]{1,0:T(8,128)(2,1)}, f32[7168,384]{1,0:T(8,128)}) fusion(bf16[7168,384]{1,0:T(8,128)(2,1)} %param.3, bf16[7168,384]{1,0:T(8,128)(2,1)} %param.2, bf16[7168,5120]{1,0:T(8,128)(2,1)} %all-gather.7.cloned.1.call-done, bf16[384,5120]{1,0:T(8,128)(2,1)} %param.1), kind=kOutput, calls=%fused_computation.13 | convolution fusion | flops 28221505536 | bytes 104857600 | tf_op jit(solution)/dot_general | solution.py:12
  278.0 45.9 %fusion.11 = bf16[7168,5120]{1,0:T(8,128)(2,1)} fusion(bf16[7168,384]{1,0:T(8,128)(2,1)} %get-tuple-element.4, bf16[5120,384]{1,0:T(8,128)(2,1)} %param.4), kind=kOutput, calls=%fused_computation.21 | convolution fusion | flops 28185722880 | bytes 82837504 | tf_op jit(solution)/dot_general | solution.py:14
  323.9 67.7 %convolution_add_fusion = bf16[7168,5120]{1,0:T(8,128)(2,1)} fusion(bf16[7168,5120]{1,0:T(8,128)(2,1)} %fusion.11, bf16[5120,384]{1,0:T(8,128)(2,1)} %param.5, f32[7168,384]{1,0:T(8,128)} %get-tuple-element.5, bf16[7168,384]{1,0:T(8,128)(2,1)} %param.3), kind=kOutput, calls=%fused_computation | convolution fusion | flops 28241690624 | bytes 167247872 | tf_op jit(solution)/dot_general | solution.py:14
  391.6 0.1 reduce-scatter.5.cloned.1.call-update
  391.6 48.3 %all-gather.9.cloned.1.call-done = bf16[7168,5120]{1,0:T(8,128)(2,1)} async-done(((bf16[224,5120]{1,0:T(8,128)(2,1)}), bf16[7168,5120]{1,0:T(8,128)(2,1)}) %all-gather.9.cloned.1.call-update) | async-done | bytes 73400336 | tf_op args[0]
  439.9 42.0 %fusion.8 = bf16[5120,384]{0,1:T(8,128)(2,1)} fusion(bf16[7168,5120]{1,0:T(8,128)(2,1)} %all-gather.9.cloned.1.call-done, f32[7168,384]{1,0:T(8,128)} %get-tuple-element.5, bf16[7168,384]{1,0:T(8,128)(2,1)} %param.3), kind=kOutput, calls=%fused_computation.19 | convolution fusion | flops 28206956544 | bytes 93847552 | tf_op jit(solution)/gta,gtb->gab/dot_general | solution.py:19
  482.0 6.3 copy.1
  488.2 38.5 %fusion.7 = bf16[5120,384]{0,1:T(8,128)(2,1)} fusion(bf16[7168,384]{1,0:T(8,128)(2,1)} %get-tuple-element.4, bf16[7168,5120]{1,0:T(8,128)(2,1)} %all-gather.9.cloned.1.call-done), kind=kOutput, calls=%fused_computation.18 | convolution fusion | flops 28187688960 | bytes 82837504 | tf_op jit(solution)/gta,gtb->gab/dot_general | solution.py:19
  526.7 6.3 copy
  533.0 42.9 %convolution_convert_fusion = bf16[384,5120]{1,0:T(8,128)(2,1)} fusion(bf16[7168,5120]{1,0:T(8,128)(2,1)} %all-gather.7.cloned.1.call-done, bf16[7168,384]{1,0:T(8,128)(2,1)} %param.2, bf16[7168,384]{1,0:T(8,128)(2,1)} %param.3), kind=kOutput, calls=%fused_computation.15 | convolution fusion | flops 28209709056 | bytes 88342528 | tf_op jit(solution)/gta,gtb->gab/dot_general | solution.py:19
  575.9 170.9 %reduce-scatter.5.cloned.1.call-done = bf16[224,5120]{1,0:T(8,128)(2,1)} async-done(((bf16[7168,5120]{1,0:T(8,128)(2,1)}), bf16[224,5120]{1,0:T(8,128)(2,1)}) %reduce-scatter.5.cloned.1.call-update) | async-done | bytes 2293776
Async XLA Ops:
  7.2 219.4 %all-gather.7.cloned.1.call-start = ((), (), s32[]{:S(2)}) async-start(), calls=%async_computation.1 | async-start | bytes 75694080 | tf_op args[1]
  8.0 432.0 %all-gather.9.cloned.1.call-start = ((), (), s32[]{:S(2)}) async-start(), calls=%async_computation.2 | async-start | bytes 75694080 | tf_op args[0]
  8.8 738.0 %reduce-scatter.5.cloned.1.call-start = ((), (), s32[]{:S(2)}) async-start(), calls=%async_computation.3 | async-start | bytes 75694080
Sparse Core Ops, SparseCore 0:
  10.1 216.4 all-gather.6
  228.7 211.1 all-gather.8
  444.5 302.1 reduce-scatter.4
where the time goes:
time: 754 us; the launch traced here: 753 us
  waiting for transfers between devices  438 us (58%)
  matrix products  288 us (38%)
  between operations  13.8 us (2%)
  local copies, waits for them, and re-layouts  12.5 us (2%)
    unnamed x6, waiting for transfers between devices  438 us
    dot_general x3, matrix products, by_group(): jnp.einsum('gta,gtb->gab', a, b, preferred_element_type=jnp.float32)  123 us
    dot_general x2, matrix products, step(): dx = jnp.dot(d_gate, w_gate.T) + jnp.dot(d_up, w_up.T)  114 us
    dot_general x1, matrix products, step(): d_hidden = jnp.dot(dy, w_down.T, preferred_element_type=jnp.float32)  51.4 us
  transfers between devices with their start and end apart: 3, of which 3 were waited for; matrix products, arithmetic and copies ran while one was open for 40% of the time, Pallas kernels for 0%

commit v1 on v0

v1 whole, which is shorter than its diff:
```python
import functools
import math

import jax
import jax.numpy as jnp
from jax import lax
from jax.experimental import pallas as pl
from jax.experimental.pallas import tpu as pltpu
from jax.sharding import PartitionSpec as P

MESH = pl.DeviceIdType.MESH
BF, F32 = jnp.bfloat16, jnp.float32
CORES = 2
AG_DY, AG_X = 0, 16
WD, GA, UP, WG, WU, R_DWD, R_DW = 32, 33, 35, 37, 38, 39, 40
RS_PAIR, RS_Y, RS_T, N_SEM = 44, 52, 58, 60
FAR_OWN, FAR_OTHER, UP_OTHER, DN_OTHER, DN_OWN, UP_OWN = range(6)


def nt(a, b):
    return lax.dot_general(a, b, (((1,), (1,)), ((), ())), preferred_element_type=F32)


def kernel(
    side,
    x, dy, gate, up, wg, wu, wd,
    dx, dwg, dwu, dwd,
    dyh, xh, tr, gub, wdb, wgub, dgu, dgut, hdt, pair_s, pair_r, acc_s, acc_r, dwd_s, dwd_r, dw_s, dw_r,
    bounce, wdv, wv, lhs, ss, rs, loc,
):
    R, D = x.shape
    F = wd.shape[0]
    H = dyh.shape[0]
    half = H // 2
    me = lax.axis_index("tp")
    dp = lax.axis_index("dp")
    k = me % CORES
    cy = (me // CORES) % side
    cx = me // (CORES * side)

    def dev(a, b, c):
        return (dp, ((a + side) % side * side + (b + side) % side) * CORES + c)

    step = 1 - 2 * k
    fx, bx = (cx + step + side) % side, (cx - step + side) % side
    yp, ym = (cy + 1) % side, (cy + side - 1) % side
    yf = (cy + 2) % side
    ahead, behind = dev(fx, cy, k), dev(bx, cy, k)
    right, left = dev(cx, yp, k), dev(cx, ym, k)
    sibling = dev(cx, cy, 1 - k)
    own, other = cx // 2, 1 - cx // 2
    par = cx % 2

    def slot(h, b, c):
        return (h * side + b) * CORES + c

    def rows(s):
        return pl.ds(pl.multiple_of(s * R, R), R)

    def copy(i, src, dst, to):
        return pltpu.make_async_remote_copy(
            src_ref=src, dst_ref=dst, send_sem=ss.at[i], recv_sem=rs.at[i], device_id=to, device_id_type=MESH
        )

    sent = []

    def send(i, src, dst, to):
        c = copy(i, src, dst, to)
        c.start()
        sent.append((i, src, dst, to))

    def arrived(i, dst):
        copy(i, dst, dst, sibling).wait_recv()

    def local(src, dst, i):
        return pltpu.make_async_copy(src, dst, loc.at[i])

    barrier = pltpu.get_barrier_semaphore()
    for to in (ahead, behind, right, left, sibling):
        pl.semaphore_signal(barrier, inc=1, device_id=to, device_id_type=MESH)
    pl.semaphore_wait(barrier, 5)

    class Gather:
        def __init__(self, base, src, buf, t):
            self.b, self.src, self.buf, self.t = base, src, buf, t

        def at(self, s):
            return self.buf.at[rows(s)]

        def pass_on(self, i, s, to):
            send(self.b + i, self.at(s), self.at(s), to)

        def start(self):
            mine = self.at(slot(own, cy, k))
            send(self.b + 0, self.src, tr.at[self.t], ahead)
            send(self.b + 2, self.src, mine, right)
            send(self.b + 3, self.src, mine, left)
            send(self.b + 8, self.src, mine, sibling)

        def e1(self):
            arrived(self.b + 0, tr.at[self.t])
            s = self.at(slot(bx // 2, cy, k))
            send(self.b + 1, tr.at[self.t], s, ahead)

        def e2(self):
            s = slot(own, ym, k)
            arrived(self.b + 2, self.at(s))
            self.pass_on(6, s, right)
            self.pass_on(10, s, sibling)

        def e3(self):
            s = slot(own, yp, k)
            arrived(self.b + 3, self.at(s))
            self.pass_on(11, s, sibling)

        def e4(self):
            s = slot(other, cy, k)
            arrived(self.b + 1, self.at(s))
            self.pass_on(4, s, right)
            self.pass_on(5, s, left)
            self.pass_on(9, s, sibling)

        def e5(self):
            s = slot(other, ym, k)
            arrived(self.b + 4, self.at(s))
            self.pass_on(12, s, sibling)

        def e6(self):
            s = slot(other, yp, k)
            arrived(self.b + 5, self.at(s))
            self.pass_on(7, s, left)
            self.pass_on(13, s, sibling)

        def e7(self):
            s = slot(own, yf, k)
            arrived(self.b + 6, self.at(s))
            self.pass_on(14, s, sibling)

        def e8(self):
            s = slot(other, yf, k)
            arrived(self.b + 7, self.at(s))
            self.pass_on(15, s, sibling)

        def finish(self):
            c = 1 - k
            for i, (h, b) in enumerate(
                ((own, cy), (other, cy), (own, ym), (own, yp), (other, ym), (other, yp), (own, yf), (other, yf))
            ):
                arrived(self.b + 8 + i, self.at(slot(h, b, c)))

    gdy, gx = Gather(AG_DY, dy, dyh, 0), Gather(AG_X, x, xh, 1)
    gdy.start()
    ins = [local(dy, bounce.at[0], 0), local(x, bounce.at[1], 1), local(wd, wdv.at[pl.ds(0, F)], 2)]
    for c in ins:
        c.start()
    ins[0].wait()
    ins[1].wait()
    mine = rows(slot(own, cy, k))
    outs = [local(bounce.at[0], dyh.at[mine], 0), local(bounce.at[1], xh.at[mine], 1)]
    for c in outs:
        c.start()
    for c in outs:
        c.wait()
    ins[2].wait()

    gdy.e1()
    send(WD, wd, wdb, ahead)
    for i in range(2):
        theirs = pl.ds(pl.multiple_of((1 - par + 2 * i) * half, half), half)
        send(GA + i, gate.at[theirs], gub.at[0, pl.ds(i * half, half)], ahead)
        send(UP + i, up.at[theirs], gub.at[1, pl.ds(i * half, half)], ahead)
    gdy.e2()
    gdy.e3()
    gdy.e4()
    gdy.e5()
    gdy.e6()
    gx.start()
    gdy.e7()
    gdy.e8()
    gdy.finish()
    arrived(WD, wdb)
    c = local(wdb, wdv.at[pl.ds(F, F)], 2)
    c.start()
    for i in range(2):
        arrived(GA + i, gub.at[0, pl.ds(i * half, half)])
        arrived(UP + i, gub.at[1, pl.ds(i * half, half)])
    c.wait()

    TA = 256

    def act(dy_v, g0, u0, g1, u1, dgu_v, dgut_v, hdt_v):
        dh = nt(dy_v[...], wdv[...])
        for s, (g_v, u_v) in enumerate(((g0, u0), (g1, u1))):
            g, u = g_v[...].astype(F32), u_v[...].astype(F32)
            d = dh[:, s * F : (s + 1) * F]
            sig = jax.nn.sigmoid(g)
            silu = g * sig
            dg = d * u * (sig + silu * (1 - sig))
            du = d * silu
            for j, v in enumerate((dg, du)):
                at = slice((2 * s + j) * F, (2 * s + j + 1) * F)
                dgu_v[:, at] = v.astype(BF)
                dgut_v[at, :] = v.T.astype(BF)
            hdt_v[s * F : (s + 1) * F, :] = (silu * u).T.astype(BF)

    def act_half(h):
        at, theirs = pl.ds(h * half, half), pl.ds(pl.multiple_of((par + 2 * h) * half, half), half)
        rowmap = lambda i: (i, 0)
        colmap = lambda i: (0, i)
        pltpu.emit_pipeline(
            act,
            grid=(half // TA,),
            in_specs=[pl.BlockSpec((TA, D), rowmap)] + [pl.BlockSpec((TA, F), rowmap)] * 4,
            out_specs=[
                pl.BlockSpec((TA, 4 * F), rowmap),
                pl.BlockSpec((4 * F, TA), colmap),
                pl.BlockSpec((2 * F, TA), colmap),
            ],
        )(
            dyh.at[at], gate.at[theirs], up.at[theirs], gub.at[0, at], gub.at[1, at],
            dgu.at[at], dgut.at[:, at], hdt.at[:, at],
        )

    act_half(0)
    gx.e1()
    send(WG, wg, wgub.at[0], ahead)
    send(WU, wu, wgub.at[1], ahead)
    act_half(1)

    gx.e2()
    gx.e3()
    gx.e4()

    TN = 512

    def dwd_part(s, got, out):
        c = local(hdt.at[pl.ds(s * F, F)], lhs.at[pl.ds(0, F)], 2)
        c.start()
        c.wait()

        def body(dy_v, *refs):
            v = jnp.dot(lhs[:F, :], dy_v[...], preferred_element_type=F32)
            for r in refs[:-1]:
                v = v + r[...].astype(F32)
            refs[-1][...] = v.astype(BF)

        col = lambda i: (0, i)
        n = 0 if got is None else 1
        pltpu.emit_pipeline(
            body,
            grid=(D // TN,),
            in_specs=[pl.BlockSpec((H, TN), col)] + [pl.BlockSpec((F, TN), col)] * n,
            out_specs=[pl.BlockSpec((F, TN), col)],
        )(dyh, *([got] if n else []), out)

    dwd_part(1, None, dwd_s)
    send(R_DWD, dwd_s, dwd_r, behind)
    gx.e5()
    gx.e6()

    arrived(WG, wgub.at[0])
    arrived(WU, wgub.at[1])
    loads = [local(w, wv.at[:, pl.ds(i * F, F)], i) for i, w in enumerate((wg, wu, wgub.at[0], wgub.at[1]))]
    for c in loads:
        c.start()
    for c in loads:
        c.wait()
    gx.e7()

    TX = 512

    def dx_part(s, adds, out):
        def body(d_v, *refs):
            n = pl.program_id(0)
            v = nt(d_v[...], wv[pl.ds(pl.multiple_of(n * TX, TX), TX), :])
            for r in refs[:-1]:
                v = v + r[...].astype(F32)
            refs[-1][...] = v.astype(BF)

        col = lambda i: (0, i)
        pltpu.emit_pipeline(
            body,
            grid=(D // TX,),
            in_specs=[pl.BlockSpec((R, 4 * F), lambda i: (0, 0))] + [pl.BlockSpec((R, TX), col)] * len(adds),
            out_specs=[pl.BlockSpec((R, TX), col)],
        )(dgu.at[rows(s)], *adds, out)

    def for_sibling(j):
        h = (own + j % 2) % 2
        dx_part(slot(h, (cy + 2 + j // 2) % side, 1 - k), (), pair_s.at[j])
        copy(RS_PAIR + j, pair_s.at[j], pair_r.at[j], sibling).start()

    def from_sibling(t, i):
        j = 2 * i + t
        arrived(RS_PAIR + j, pair_r.at[j])
        return pair_r.at[j]

    def pass_sum(n, h, b, t, i, adds, to):
        dx_part(slot(h, b, k), (from_sibling(t, i), *adds), acc_s.at[n])
        send(RS_Y + n, acc_s.at[n], acc_r.at[n], to)

    def got(n):
        arrived(RS_Y + n, acc_r.at[n])
        return acc_r.at[n]

    lax.fori_loop(0, 2, lambda j, _: (for_sibling(j), 0)[1], 0)
    pass_sum(FAR_OWN, own, yf, 0, 0, (), right)
    pass_sum(FAR_OTHER, other, yf, 1, 0, (), left)
    gx.e8()
    gx.finish()

    cols = D // 2

    def dw_part(s, q, adds, outs):
        def body(x_v, *refs):
            v = jnp.dot(lhs[...], x_v[...], preferred_element_type=F32)
            for i in range(2):
                a = v[i * F : (i + 1) * F].T
                if adds:
                    a = a + refs[i][...].astype(F32)
                refs[len(adds) + i][...] = a.astype(BF)

        row = lambda i: (i, 0)
        pltpu.emit_pipeline(
            body,
            grid=(cols // TN,),
            in_specs=[pl.BlockSpec((H, TN), lambda i: (0, q * (cols // TN) + i))]
            + [pl.BlockSpec((TN, F), row)] * len(adds),
            out_specs=[pl.BlockSpec((TN, F), row)] * 2,
        )(xh, *adds, *outs)

    def load_lhs(s):
        c = local(dgut.at[pl.ds(s * 2 * F, 2 * F)], lhs, 2)
        c.start()
        c.wait()

    load_lhs(1)
    for q in range(2):
        dw_part(1, q, (), [dw_s.at[q, i] for i in range(2)])
        for i in range(2):
            send(R_DW + 2 * q + i, dw_s.at[q, i], dw_r.at[q, i], behind)
    lax.fori_loop(2, 8, lambda j, _: (for_sibling(j), 0)[1], 0)
    pass_sum(UP_OTHER, other, yp, 1, 3, (), right)
    pass_sum(DN_OTHER, other, ym, 1, 1, (got(FAR_OTHER),), left)
    pass_sum(DN_OWN, own, ym, 0, 1, (), left)
    pass_sum(UP_OWN, own, yp, 0, 3, (got(FAR_OWN),), right)
    arrived(R_DWD, dwd_r)
    dwd_part(0, dwd_r, dwd)
    dx_part(slot(other, cy, k), (from_sibling(1, 2), got(UP_OTHER), got(DN_OTHER)), acc_s.at[6])
    send(RS_T, acc_s.at[6], tr.at[2], ahead)
    load_lhs(0)
    for q in range(2):
        for i in range(2):
            arrived(R_DW + 2 * q + i, dw_r.at[q, i])
        dw_part(0, q, [dw_r.at[q, i] for i in range(2)], [w.at[pl.ds(q * cols, cols)] for w in (dwg, dwu)])
        if q == 0:
            arrived(RS_T, tr.at[2])
            send(RS_T + 1, tr.at[2], acc_r.at[6], ahead)
    arrived(RS_T + 1, acc_r.at[6])
    dx_part(slot(own, cy, k), (from_sibling(0, 2), got(UP_OWN), got(DN_OWN), acc_r.at[6]), dx)

    for a in sent:
        copy(*a).wait_send()
    for j in range(8):
        copy(RS_PAIR + j, pair_s.at[j], pair_r.at[j], sibling).wait_send()


def solution(mesh):
    side = math.isqrt(mesh.shape["tp"] // CORES)

    def body(x, dy, gate, up, w_gate, w_up, w_down):
        R, D = x.shape
        F = w_down.shape[0]
        H = gate.shape[0] // 2
        S = jax.ShapeDtypeStruct
        shapes = [
            S((R, D), BF), S((D, F), BF), S((D, F), BF), S((F, D), BF),
            S((H, D), BF), S((H, D), BF), S((3, R, D), BF), S((2, H, F), BF), S((F, D), BF), S((2, D, F), BF),
            S((H, 4 * F), BF), S((4 * F, H), BF), S((2 * F, H), BF),
            S((8, R, D), BF), S((8, R, D), BF), S((7, R, D), BF), S((7, R, D), BF),
            S((F, D), BF), S((F, D), BF), S((2, 2, D // 2, F), BF), S((2, 2, D // 2, F), BF),
        ]
        any_ = pl.BlockSpec(memory_space=pl.ANY)
        outs = pl.pallas_call(
            functools.partial(kernel, side),
            out_shape=shapes,
            in_specs=[any_] * 7,
            out_specs=[any_] * len(shapes),
            scratch_shapes=[
                pltpu.VMEM((2, R, D), BF),
                pltpu.VMEM((2 * F, D), BF),
                pltpu.VMEM((D, 4 * F), BF),
                pltpu.VMEM((2 * F, H), BF),
                pltpu.SemaphoreType.DMA((N_SEM,)),
                pltpu.SemaphoreType.DMA((N_SEM,)),
                pltpu.SemaphoreType.DMA((4,)),
            ],
            compiler_params=pltpu.CompilerParams(
                collective_id=0, has_side_effects=True, vmem_limit_bytes=62 * 1024 * 1024
            ),
        )(x, dy, gate, up, w_gate, w_up, w_down)
        return tuple(outs[:4])

    rows, cols, own = P(("dp", "tp"), None), P("dp", "tp"), P(None, "tp")
    return jax.shard_map(
        body,
        mesh=mesh,
        in_specs=(rows, rows, cols, cols, own, own, P("tp", None)),
        out_specs=(rows, cols, cols, P(("dp", "tp"), None)),
        check_vma=False,
    )
```

time: 754 us -> 702 us (0.931)
  Pallas kernels: 0 us -> 687 us
  waiting for transfers between devices: 438 us -> 0 us
  matrix products: 288 us -> 0 us
  between operations: 13.8 us -> 0.66 us
    pallas_call x0 -> x1, Pallas kernels: none -> 687 us  [body(): pl.pallas_call(functools.partial(kernel, side), out_shape=shapes, in_spec...]
    unnamed x6 -> x0, waiting for transfers between devices: 438 us -> none
    dot_general x6 -> x0, matrix products: 288 us -> none  [the longest x3 123 us: by_group(): jnp.einsum('gta,gtb->gab', a, b, preferred_element_type=jnp.float32)]
  transfers between devices with their start and end apart: 3 -> 0, of which waited for: 3 -> 0; matrix products, arithmetic and copies ran while one was open for 40% -> 0% of each run, Pallas kernels for 0% -> 0%
where the time goes in v1:
time: 702 us; the launch traced here: 699 us
  Pallas kernels  687 us (98%)
  local copies, waits for them, and re-layouts  11.4 us (2%)
    pallas_call x1, Pallas kernels, body(): pl.pallas_call(functools.partial(kernel, side), out_shape=shapes, in_spec...  687 us

profile of v1, /device:TPU:97, one launch (start us, length us, event | category | flops | bytes accessed | tf_op | source)
XLA Modules:
  0.0 699.0 jit_solution(2599013396514873549)
XLA Ops:
  0.6 687.0 %shard_map.102 = (bf16[224,5120]{1,0:T(8,128)(2,1)}, bf16[5120,384]{1,0:T(8,128)(2,1)}, bf16[5120,384]{1,0:T(8,128)(2,1)}, bf16[384,5120]{1,0:T(8,128)(2,1)}, bf...) custom-call(bf16[224,5120]{1,0:T(8,128)(2,1)} %x.1, ...), custom_call_target="tpu_custom_call" | custom-call | tf_op jit(solution)/shard_map/pallas_call | solution.py:384
  687.6 0.0 copy-start.2
  687.6 0.0 copy-start.1
  687.6 3.3 copy.15
  690.9 0.0 copy-done.2
  690.9 1.9 copy.16
  692.9 0.7 copy-done.1
  693.5 0.0 copy-start
  693.5 2.0 copy.17
  695.5 1.5 copy-done
  697.1 1.9 copy.18
Async XLA Ops:
  687.6 3.4 copy-start.2
  687.6 5.9 copy-start.1
  693.5 3.5 copy-start

commit v2 on v1

v2 whole, which is shorter than its diff:
```python
import functools
import math

import jax
import jax.numpy as jnp
from jax import lax
from jax.experimental import pallas as pl
from jax.experimental.pallas import tpu as pltpu
from jax.sharding import PartitionSpec as P

MESH = pl.DeviceIdType.MESH
BF, F32 = jnp.bfloat16, jnp.float32
CORES = 2
AG_DY, AG_X = 0, 16
WD, GA, UP, WG, WU, R_DWD, R_DW = 32, 33, 35, 37, 38, 39, 40
RS_PAIR, RS_Y, RS_T, N_SEM = 44, 52, 58, 62
FAR_OWN, FAR_OTHER, UP_OTHER, DN_OTHER, DN_OWN, UP_OWN = range(6)


def nt(a, b):
    return lax.dot_general(a, b, (((1,), (1,)), ((), ())), preferred_element_type=F32)


def kernel(
    side,
    x, dy, gate, up, wg, wu, wd,
    dwg, dwu,
    dyh, xh, tr, own_gu, gub, wdb, wgub, dgu, dgut, hdt, pair_s, pair_r, acc_s, acc_r, part, dwd_s, dwd_r, dwd_f, dw_s, dw_r, dw_f,
    wv, wdt, lhs, ss, rs, loc,
):
    R, D = x.shape
    F = wd.shape[0]
    H = dyh.shape[0]
    half = H // 2
    me = lax.axis_index("tp")
    dp = lax.axis_index("dp")
    k = me % CORES
    cy = (me // CORES) % side
    cx = me // (CORES * side)

    def dev(a, b, c):
        return (dp, ((a + side) % side * side + (b + side) % side) * CORES + c)

    step = 1 - 2 * k
    fx, bx = (cx + step + side) % side, (cx - step + side) % side
    yp, ym = (cy + 1) % side, (cy + side - 1) % side
    yf = (cy + 2) % side
    ahead, behind = dev(fx, cy, k), dev(bx, cy, k)
    right, left = dev(cx, yp, k), dev(cx, ym, k)
    sibling = dev(cx, cy, 1 - k)
    own, other = cx // 2, 1 - cx // 2
    par = cx % 2

    def slot(h, b, c):
        return (h * side + b) * CORES + c

    def rows(s):
        return pl.ds(pl.multiple_of(s * R, R), R)

    def copy(i, src, dst, to):
        return pltpu.make_async_remote_copy(
            src_ref=src, dst_ref=dst, send_sem=ss.at[i], recv_sem=rs.at[i], device_id=to, device_id_type=MESH
        )

    def half_of(h):
        return pl.ds(pl.multiple_of(h * half, half), half)

    sent = []

    def send(i, src, dst, to):
        c = copy(i, src, dst, to)
        c.start()
        sent.append((i, src, dst, to))

    def arrived(i, dst):
        copy(i, dst, dst, sibling).wait_recv()

    def local(src, dst, i):
        return pltpu.make_async_copy(src, dst, loc.at[i])

    barrier = pltpu.get_barrier_semaphore()
    for to in (ahead, behind, right, left, sibling):
        pl.semaphore_signal(barrier, inc=1, device_id=to, device_id_type=MESH)
    pl.semaphore_wait(barrier, 5)

    class Gather:
        def __init__(self, base, src, buf, t):
            self.b, self.src, self.buf, self.t = base, src, buf, t

        def at(self, s):
            return self.buf.at[rows(s)]

        def pass_on(self, i, s, to):
            send(self.b + i, self.at(s), self.at(s), to)

        def start(self):
            mine = self.at(slot(own, cy, k))
            send(self.b + 0, self.src, tr.at[self.t], ahead)
            send(self.b + 2, self.src, mine, right)
            send(self.b + 3, self.src, mine, left)
            send(self.b + 8, self.src, mine, sibling)

        def e1(self):
            arrived(self.b + 0, tr.at[self.t])
            s = self.at(slot(bx // 2, cy, k))
            send(self.b + 1, tr.at[self.t], s, ahead)

        def e2(self):
            s = slot(own, ym, k)
            arrived(self.b + 2, self.at(s))
            self.pass_on(6, s, right)
            self.pass_on(10, s, sibling)

        def e3(self):
            s = slot(own, yp, k)
            arrived(self.b + 3, self.at(s))
            self.pass_on(11, s, sibling)

        def e4(self):
            s = slot(other, cy, k)
            arrived(self.b + 1, self.at(s))
            self.pass_on(4, s, right)
            self.pass_on(5, s, left)
            self.pass_on(9, s, sibling)

        def e5(self):
            s = slot(other, ym, k)
            arrived(self.b + 4, self.at(s))
            self.pass_on(12, s, sibling)

        def e6(self):
            s = slot(other, yp, k)
            arrived(self.b + 5, self.at(s))
            self.pass_on(7, s, left)
            self.pass_on(13, s, sibling)

        def e7(self):
            s = slot(own, yf, k)
            arrived(self.b + 6, self.at(s))
            self.pass_on(14, s, sibling)

        def e8(self):
            s = slot(other, yf, k)
            arrived(self.b + 7, self.at(s))
            self.pass_on(15, s, sibling)

        def finish_half(self, n):
            h = (own, other)[n]
            for i, b in zip(((8, 10, 11, 14), (9, 12, 13, 15))[n], (cy, ym, yp, yf)):
                arrived(self.b + i, self.at(slot(h, b, 1 - k)))

    gdy, gx = Gather(AG_DY, dy, dyh, 0), Gather(AG_X, x, xh, 1)
    gdy.start()

    rowmap = lambda i: (i, 0)
    colmap = lambda i: (0, i)
    TX = 1024

    def through(pairs, *shape):
        def go(buf):
            for leg in range(2):
                cs = [
                    local(*((buf.at[i], dst) if leg else (src, buf.at[i])), i) for i, (src, dst) in enumerate(pairs)
                ]
                for c in cs:
                    c.start()
                for c in cs:
                    c.wait()

        pl.run_scoped(go, pltpu.VMEM((len(pairs), *shape), BF))

    def turn_w(w, r):
        def body(t):
            at = pl.ds(pl.multiple_of(pl.program_id(0) * TX, TX), TX)
            wv[pl.ds(r * F, F), at] = t[...].T

        pltpu.emit_pipeline(body, grid=(D // TX,), in_specs=[pl.BlockSpec((TX, F), rowmap)])(w)

    def turn_wd(w, r):
        def body(t):
            at = pl.ds(pl.multiple_of(pl.program_id(0) * TX, TX), TX)
            wdt[at, pl.ds(r * F, F)] = t[...].T

        pltpu.emit_pipeline(body, grid=(D // TX,), in_specs=[pl.BlockSpec((F, TX), colmap)])(w)

    mine = rows(slot(own, cy, k))
    through([(dy, dyh.at[mine]), (x, xh.at[mine])], R, D)

    gdy.e1()
    send(WD, wd, wdb, ahead)
    for i in range(2):
        h = (fx // 2 + i) % 2
        theirs = pl.ds(pl.multiple_of((1 - par + 2 * h) * half, half), half)
        send(GA + i, gate.at[theirs], gub.at[0, half_of(h)], ahead)
        send(UP + i, up.at[theirs], gub.at[1, half_of(h)], ahead)
    turn_wd(wd, 0)
    gdy.e2()
    gdy.e3()
    gdy.e4()
    ours = [pl.ds(pl.multiple_of((par + 2 * i) * half, half), half) for i in range(2)]
    through([(a.at[ours[i]], own_gu.at[j, pl.ds(i * half, half)]) for j, a in enumerate((gate, up)) for i in range(2)], half, F)
    turn_w(wg, 0)
    turn_w(wu, 1)
    gdy.e6()
    gx.start()
    gdy.e7()
    arrived(WD, wdb)
    turn_wd(wdb, 1)
    TA = 256

    def act(dy_v, g0, u0, g1, u1, dgu_v, dgut_v, hdt_v):
        dh = jnp.dot(dy_v[...], wdt[...], preferred_element_type=F32)
        for s, (g_v, u_v) in enumerate(((g0, u0), (g1, u1))):
            g, u = g_v[...].astype(F32), u_v[...].astype(F32)
            d = dh[:, s * F : (s + 1) * F]
            sig = jax.nn.sigmoid(g)
            silu = g * sig
            dg = d * u * (sig + silu * (1 - sig))
            du = d * silu
            for j, v in enumerate((dg, du)):
                to = pl.ds((2 * s + j) * F, F)
                dgu_v[:, to] = v.astype(BF)
                dgut_v[to, :] = v.T.astype(BF)
            hdt_v[pl.ds(s * F, F), :] = (silu * u).T.astype(BF)

    def act_half(i, h):
        arrived(GA + i, gub.at[0, half_of(h)])
        arrived(UP + i, gub.at[1, half_of(h)])
        at = half_of(h)
        pltpu.emit_pipeline(
            act,
            grid=(half // TA,),
            in_specs=[pl.BlockSpec((TA, D), rowmap)] + [pl.BlockSpec((TA, F), rowmap)] * 4,
            out_specs=[
                pl.BlockSpec((TA, 4 * F), rowmap),
                pl.BlockSpec((4 * F, TA), colmap),
                pl.BlockSpec((2 * F, TA), colmap),
            ],
        )(
            dyh.at[at], own_gu.at[0, at], own_gu.at[1, at], gub.at[0, at], gub.at[1, at],
            dgu.at[at], dgut.at[:, at], hdt.at[:, at],
        )

    gdy.finish_half(0)
    act_half(0, own)
    gdy.e5()
    gdy.e8()
    gdy.finish_half(1)
    act_half(1, other)
    gx.e1()
    send(WG, wg, wgub.at[0], ahead)
    send(WU, wu, wgub.at[1], ahead)

    TN, WIDE = 512, 1024

    def load_lhs(src, r, n, halves=(0, 1)):
        cs = [
            local(src.at[pl.ds(r, n), pl.ds(pl.multiple_of(h * half, half), half)], lhs.at[i, pl.ds(0, n)], i)
            for i, h in enumerate(halves)
        ]
        for c in cs:
            c.start()
        for c in cs:
            c.wait()

    def dwd_part(out):
        def body(dy_v, o_v):
            v = jnp.dot(lhs[0, :F, :], dy_v[:half, :], preferred_element_type=F32)
            v += jnp.dot(lhs[1, :F, :], dy_v[half:, :], preferred_element_type=F32)
            o_v[...] = v.astype(o_v.dtype)

        pltpu.emit_pipeline(
            body,
            grid=(D // WIDE,),
            in_specs=[pl.BlockSpec((H, WIDE), colmap)],
            out_specs=[pl.BlockSpec((F, WIDE), colmap)],
        )(dyh, out)

    load_lhs(hdt, F, F)
    dwd_part(dwd_s)
    gx.e2()
    gx.e3()
    gx.e4()
    load_lhs(hdt, 0, F)
    dwd_part(dwd_f)
    arrived(WG, wgub.at[0])
    turn_w(wgub.at[0], 2)
    gx.e6()
    gx.e7()
    gx.finish_half(0)

    cols = D // 2

    def dw_half(i, h, q, n, tn, adds, outs):
        def body(x_v, *refs):
            v = jnp.dot(lhs[i], x_v[...], preferred_element_type=F32)
            for j in range(2):
                a = v[j * F : (j + 1) * F].T
                if adds:
                    a = a + refs[j][...]
                refs[len(adds) + j][...] = a.astype(refs[len(adds) + j].dtype)

        pltpu.emit_pipeline(
            body,
            grid=(n // tn,),
            in_specs=[pl.BlockSpec((half, tn), colmap)] + [pl.BlockSpec((tn, F), rowmap)] * len(adds),
            out_specs=[pl.BlockSpec((tn, F), rowmap)] * 2,
        )(xh.at[pl.ds(pl.multiple_of(h * half, half), half), pl.ds(q * n, n)], *adds, *outs)

    load_lhs(dgut, 2 * F, 2 * F, (own, other))
    dw_half(0, own, 0, D, WIDE, (), [dw_f.at[0], dw_f.at[1]])

    arrived(WU, wgub.at[1])
    send(R_DWD, dwd_s, dwd_r, behind)
    turn_w(wgub.at[1], 3)

    def dx_blocks(slots, adds, outs):
        m = len(slots)
        n_adds = sum(map(len, adds))

        def body(*refs):
            n = pl.program_id(0)
            d = jnp.concatenate([r[...] for r in refs[:m]], axis=0)
            at = pl.ds(pl.multiple_of(n * TX, TX), TX)
            v = jnp.dot(d, wv[:, at], preferred_element_type=F32)
            terms = iter(refs[m : m + n_adds])
            for j in range(m):
                a = v[j * R : (j + 1) * R]
                for _ in adds[j]:
                    a = a + next(terms)[...].astype(F32)
                o = refs[m + n_adds + j]
                o[...] = a.astype(o.dtype)

        tile = pl.BlockSpec((R, TX), colmap)
        pltpu.emit_pipeline(
            body,
            grid=(D // TX,),
            in_specs=[pl.BlockSpec((R, 4 * F), lambda i: (0, 0))] * m + [tile] * n_adds,
            out_specs=[tile] * m,
        )(*[dgu.at[rows(q)] for q in slots], *[a for b in adds for a in b], *outs)

    def dx_pairs(ys, c, adds, outs):
        dx_blocks([slot(h, b, c) for b in ys for h in (own, other)], adds, outs)

    def for_sibling(*ns):
        js = [2 * i + t for i in ns for t in range(2)]
        dx_pairs([(cy + 2 + i) % side for i in ns], 1 - k, [()] * len(js), [pair_s.at[j] for j in js])
        for j in js:
            send(RS_PAIR + j, pair_s.at[j], pair_r.at[j], sibling)

    def from_sibling(i):
        for j in (2 * i, 2 * i + 1):
            arrived(RS_PAIR + j, pair_r.at[j])
        return [(pair_r.at[2 * i],), (pair_r.at[2 * i + 1],)]

    def add(srcs, out):
        def body(*refs):
            v = refs[0][...]
            for r in refs[1:-1]:
                v = v + r[...].astype(F32)
            refs[-1][...] = v.astype(refs[-1].dtype)

        tile = pl.BlockSpec((32, D), rowmap)
        pltpu.emit_pipeline(body, grid=(R // 32,), in_specs=[tile] * len(srcs), out_specs=[tile])(*srcs, out)

    def got(n):
        arrived(RS_Y + n, acc_r.at[n])
        return acc_r.at[n]

    def pass_sum(n, to):
        send(RS_Y + n, acc_s.at[n], acc_r.at[n], to)

    for_sibling(0)
    gx.e5()
    gx.e8()
    dx_pairs([yf], k, from_sibling(0), [acc_s.at[FAR_OWN], acc_s.at[FAR_OTHER]])
    pass_sum(FAR_OWN, right)
    pass_sum(FAR_OTHER, left)
    gx.finish_half(1)

    def dw_rest(q):
        dw_half(1, other, q, cols, TN, [dw_f.at[i, pl.ds(q * cols, cols)] for i in range(2)], [dw_s.at[q, i] for i in range(2)])
        for i in range(2):
            send(R_DW + 2 * q + i, dw_s.at[q, i], dw_r.at[q, i], behind)

    dw_rest(0)
    for_sibling(1, 3)
    dw_rest(1)
    dx_pairs(
        [ym, yp], k, from_sibling(1) + from_sibling(3),
        [acc_s.at[DN_OWN], part.at[0], part.at[1], acc_s.at[UP_OTHER]],
    )
    pass_sum(UP_OTHER, right)
    add([part.at[0], got(FAR_OTHER)], acc_s.at[DN_OTHER])
    pass_sum(DN_OTHER, left)
    pass_sum(DN_OWN, left)
    add([part.at[1], got(FAR_OWN)], acc_s.at[UP_OWN])
    pass_sum(UP_OWN, right)
    for_sibling(2)

    def dw_own(q, lo, n):
        adds = [dw_r.at[q, i] for i in range(2)]
        if lo == 0:
            for i in range(2):
                arrived(R_DW + 2 * q + i, adds[i])

        def body(x_v, g_r, u_r, g_o, u_o):
            v = jnp.dot(lhs[0], x_v[:half, :], preferred_element_type=F32)
            v += jnp.dot(lhs[1], x_v[half:, :], preferred_element_type=F32)
            for j, (r, o) in enumerate(((g_r, g_o), (u_r, u_o))):
                o[...] = (v[j * F : (j + 1) * F].T + r[...].astype(F32)).astype(BF)

        at, part_ = pl.ds(q * cols + lo * TN, n * TN), pl.ds(lo * TN, n * TN)
        pltpu.emit_pipeline(
            body,
            grid=(n,),
            in_specs=[pl.BlockSpec((H, TN), colmap)] + [pl.BlockSpec((TN, F), rowmap)] * 2,
            out_specs=[pl.BlockSpec((TN, F), rowmap)] * 2,
        )(xh.at[:, at], *[a.at[part_] for a in adds], dwg.at[at], dwu.at[at])

    parts = [pl.ds(i * (R // 2), R // 2) for i in range(2)]

    def onward(i):
        arrived(RS_T + i, tr.at[2, parts[i]])
        send(RS_T + 2 + i, tr.at[2, parts[i]], acc_r.at[6, parts[i]], ahead)

    load_lhs(dgut, 0, 2 * F)
    tiles = cols // TN
    most = tiles - tiles // 2
    dw_own(0, 0, most)
    dx_pairs([cy], k, from_sibling(2), [part.at[2], part.at[3]])
    add([part.at[3], got(UP_OTHER), got(DN_OTHER)], acc_s.at[6])
    for i in range(2):
        send(RS_T + i, acc_s.at[6, parts[i]], tr.at[2, parts[i]], ahead)
    dw_own(0, most, tiles - most)
    onward(0)
    dw_own(1, 0, most)
    onward(1)
    dw_own(1, most, tiles - most)
    arrived(R_DWD, dwd_r)
    got(UP_OWN)
    got(DN_OWN)
    for i in range(2):
        arrived(RS_T + 2 + i, acc_r.at[6, parts[i]])

    for a in sent:
        copy(*a).wait_send()


def solution(mesh):
    side = math.isqrt(mesh.shape["tp"] // CORES)

    def body(x, dy, gate, up, w_gate, w_up, w_down):
        R, D = x.shape
        F = w_down.shape[0]
        H = gate.shape[0] // 2
        S = jax.ShapeDtypeStruct
        shapes = [
            S((D, F), BF), S((D, F), BF),
            S((H, D), BF), S((H, D), BF), S((3, R, D), BF), S((2, H, F), BF), S((2, H, F), BF), S((F, D), BF), S((2, D, F), BF),
            S((H, 4 * F), BF), S((4 * F, H), BF), S((2 * F, H), BF),
            S((8, R, D), BF), S((8, R, D), BF), S((7, R, D), BF), S((7, R, D), BF), S((4, R, D), F32),
            S((F, D), BF), S((F, D), BF), S((F, D), F32), S((2, 2, D // 2, F), BF), S((2, 2, D // 2, F), BF), S((2, D, F), F32),
        ]
        any_ = pl.BlockSpec(memory_space=pl.ANY)
        outs = pl.pallas_call(
            functools.partial(kernel, side),
            out_shape=shapes,
            in_specs=[any_] * 7,
            out_specs=[any_] * len(shapes),
            scratch_shapes=[
                pltpu.VMEM((4 * F, D), BF),
                pltpu.VMEM((D, 2 * F), BF),
                pltpu.VMEM((2, 2 * F, H // 2), BF),
                pltpu.SemaphoreType.DMA((N_SEM,)),
                pltpu.SemaphoreType.DMA((N_SEM,)),
                pltpu.SemaphoreType.DMA((8,)),
            ],
            compiler_params=pltpu.CompilerParams(
                collective_id=0, has_side_effects=True, vmem_limit_bytes=67_000_000
            ),
        )(x, dy, gate, up, w_gate, w_up, w_down)
        dwg, dwu = outs[:2]
        acc_r, part, _, dwd_r, dwd_f = outs[15:20]
        dx = part[2] + sum(acc_r[n].astype(F32) for n in (UP_OWN, DN_OWN, 6))
        dwd = dwd_f + dwd_r.astype(F32)
        return dx.astype(BF), dwg, dwu, dwd.astype(BF)

    rows, cols, own = P(("dp", "tp"), None), P("dp", "tp"), P(None, "tp")
    return jax.shard_map(
        body,
        mesh=mesh,
        in_specs=(rows, rows, cols, cols, own, own, P("tp", None)),
        out_specs=(rows, cols, cols, P(("dp", "tp"), None)),
        check_vma=False,
    )
```

time: 702 us -> 545 us (0.78)
  Pallas kernels: 687 us -> 523 us
  other arithmetic: 0 us -> 9.5 us
    pallas_call x1, Pallas kernels: 687 us -> 523 us  [body(): pl.pallas_call(functools.partial(kernel, side), out_shape=shapes, in_spec...]
where the time goes in v2:
time: 545 us; the launch traced here: 541 us
  Pallas kernels  523 us (96%)
  other arithmetic  9.5 us (2%)
  local copies, waits for them, and re-layouts  7.65 us (1%)
    pallas_call x1, Pallas kernels, body(): pl.pallas_call(functools.partial(kernel, side), out_shape=shapes, in_spec...  523 us

profile of v2, /device:TPU:97, one launch (start us, length us, event | category | flops | bytes accessed | tf_op | source)
XLA Modules:
  0.0 541.2 jit_solution(13057805743248361213)
XLA Ops:
  0.6 523.4 %shard_map.102 = (bf16[5120,384]{1,0:T(8,128)(2,1)}, bf16[5120,384]{1,0:T(8,128)(2,1)}, bf16[3584,5120]{1,0:T(8,128)(2,1)}, bf16[3584,5120]{1,0:T(8,128)(2,1)}, ...) custom-call(bf16[224,5120]{1,0:T(8,128)(2,1)} %x.1, ...), custom_call_target="tpu_custom_call" | custom-call | tf_op jit(solution)/shard_map/pallas_call | solution.py:466
  524.0 0.0 copy-start
  524.1 0.0 copy-start.3
  524.1 6.3 %fusion = bf16[224,5120]{1,0:T(8,128)(2,1)} fusion(f32[4,224,5120]{2,1,0:T(8,128)} %get-tuple-element.10, bf16[7,224,5120]{2,1,0:T(8,128)(2,1)} %get-tuple-element.11), kind=kLoop, calls=%fused_computation.2 | loop fusion | flops 8028160 | bytes 13762560 | tf_op jit(solution)/shard_map/add | solution.py:485
  530.4 1.1 copy-done
  531.5 1.1 copy-done.3
  532.6 0.0 copy-start.2
  532.6 3.2 add_convert_fusion
  535.8 0.0 copy-done.2
  535.8 0.0 copy-start.1
  535.8 2.0 copy.13
  537.8 1.5 copy-done.1
  539.3 1.9 copy.14
Async XLA Ops:
  524.0 7.4 %copy-start = (f32[384,5120]{1,0:T(8,128)S(1)}, f32[384,5120]{1,0:T(8,128)}, u32[]{:S(2)}) copy-start(f32[384,5120]{1,0:T(8,128)} %get-tuple-element.14) | copy-start | bytes 23592964
  524.1 8.5 %copy-start.3 = (bf16[384,5120]{1,0:T(8,128)(2,1)S(1)}, bf16[384,5120]{1,0:T(8,128)(2,1)}, u32[]{:S(2)}) copy-start(bf16[384,5120]{1,0:T(8,128)(2,1)} %get-tuple-element.15) | copy-start | bytes 11796484
  532.6 3.2 copy-start.2
  535.8 3.5 copy-start.1

commit v3 on v2

--- a/solution.py
+++ b/solution.py
@@ -283,6 +283,43 @@
     gx.e4()
     load_lhs(hdt, 0, F)
     dwd_part(dwd_f)
+    def dx_blocks(slots, adds, outs, depth=None):
+        first, width = (0, 4 * F) if depth is None else (depth, 2 * F)
+        m = len(slots)
+        n_adds = sum(map(len, adds))
+
+        def body(*refs):
+            n = pl.program_id(0)
+            d = jnp.concatenate([r[...] for r in refs[:m]], axis=0)
+            at = pl.ds(pl.multiple_of(n * TX, TX), TX)
+            v = jnp.dot(d, wv[pl.ds(first * width, width), at], preferred_element_type=F32)
+            terms = iter(refs[m : m + n_adds])
+            for j in range(m):
+                a = v[j * R : (j + 1) * R]
+                for _ in adds[j]:
+                    a = a + next(terms)[...].astype(F32)
+                o = refs[m + n_adds + j]
+                o[...] = a.astype(o.dtype)
+
+        tile = pl.BlockSpec((R, TX), colmap)
+        pltpu.emit_pipeline(
+            body,
+            grid=(D // TX,),
+            in_specs=[pl.BlockSpec((R, width), lambda i: (0, first))] * m + [tile] * n_adds,
+            out_specs=[tile] * m,
+        )(*[dgu.at[rows(q)] for q in slots], *[a for b in adds for a in b], *outs)
+
+    def dx_pairs(ys, c, adds, outs, depth=None):
+        dx_blocks([slot(h, b, c) for b in ys for h in (own, other)], adds, outs, depth)
+
+    def for_sibling(*ns, adds=None, depth=None):
+        js = [2 * i + t for i in ns for t in range(2)]
+        dx_pairs([(cy + 2 + i) % side for i in ns], 1 - k, adds or [()] * len(js), [pair_s.at[j] for j in js], depth)
+        for j in js:
+            send(RS_PAIR + j, pair_s.at[j], pair_r.at[j], sibling)
+
+    dx_pairs([yf], 1 - k, [(), ()], [part.at[0], part.at[1]], 0)
+    dx_pairs([yf], k, [(), ()], [part.at[2], part.at[3]], 0)
     arrived(WG, wgub.at[0])
     turn_w(wgub.at[0], 2)
     gx.e6()
@@ -314,40 +351,6 @@
     send(R_DWD, dwd_s, dwd_r, behind)
     turn_w(wgub.at[1], 3)
 
-    def dx_blocks(slots, adds, outs):
-        m = len(slots)
-        n_adds = sum(map(len, adds))
-
-        def body(*refs):
-            n = pl.program_id(0)
-            d = jnp.concatenate([r[...] for r in refs[:m]], axis=0)
-            at = pl.ds(pl.multiple_of(n * TX, TX), TX)
-            v = jnp.dot(d, wv[:, at], preferred_element_type=F32)
-            terms = iter(refs[m : m + n_adds])
-            for j in range(m):
-                a = v[j * R : (j + 1) * R]
-                for _ in adds[j]:
-                    a = a + next(terms)[...].astype(F32)
-                o = refs[m + n_adds + j]
-                o[...] = a.astype(o.dtype)
-
-        tile = pl.BlockSpec((R, TX), colmap)
-        pltpu.emit_pipeline(
-            body,
-            grid=(D // TX,),
-            in_specs=[pl.BlockSpec((R, 4 * F), lambda i: (0, 0))] * m + [tile] * n_adds,
-            out_specs=[tile] * m,
-        )(*[dgu.at[rows(q)] for q in slots], *[a for b in adds for a in b], *outs)
-
-    def dx_pairs(ys, c, adds, outs):
-        dx_blocks([slot(h, b, c) for b in ys for h in (own, other)], adds, outs)
-
-    def for_sibling(*ns):
-        js = [2 * i + t for i in ns for t in range(2)]
-        dx_pairs([(cy + 2 + i) % side for i in ns], 1 - k, [()] * len(js), [pair_s.at[j] for j in js])
-        for j in js:
-            send(RS_PAIR + j, pair_s.at[j], pair_r.at[j], sibling)
-
     def from_sibling(i):
         for j in (2 * i, 2 * i + 1):
             arrived(RS_PAIR + j, pair_r.at[j])
@@ -370,10 +373,13 @@
     def pass_sum(n, to):
         send(RS_Y + n, acc_s.at[n], acc_r.at[n], to)
 
-    for_sibling(0)
+    for_sibling(0, adds=[(part.at[0],), (part.at[1],)], depth=1)
     gx.e5()
     gx.e8()
-    dx_pairs([yf], k, from_sibling(0), [acc_s.at[FAR_OWN], acc_s.at[FAR_OTHER]])
+    dx_pairs(
+        [yf], k, [(part.at[2 + t], *a) for t, a in enumerate(from_sibling(0))],
+        [acc_s.at[FAR_OWN], acc_s.at[FAR_OTHER]], 1,
+    )
     pass_sum(FAR_OWN, right)
     pass_sum(FAR_OTHER, left)
     gx.finish_half(1)
@@ -396,8 +402,6 @@
     pass_sum(DN_OWN, left)
     add([part.at[1], got(FAR_OWN)], acc_s.at[UP_OWN])
     pass_sum(UP_OWN, right)
-    for_sibling(2)
-
     def dw_own(q, lo, n):
         adds = [dw_r.at[q, i] for i in range(2)]
         if lo == 0:
@@ -418,25 +422,26 @@
             out_specs=[pl.BlockSpec((TN, F), rowmap)] * 2,
         )(xh.at[:, at], *[a.at[part_] for a in adds], dwg.at[at], dwu.at[at])
 
+    tiles = cols // TN
+    few = tiles // 2
+    for_sibling(2)
+    load_lhs(dgut, 0, 2 * F)
+    dw_own(0, 0, few)
+    dx_pairs([cy], k, from_sibling(2), [part.at[2], part.at[3]])
+
     parts = [pl.ds(i * (R // 2), R // 2) for i in range(2)]
 
     def onward(i):
         arrived(RS_T + i, tr.at[2, parts[i]])
         send(RS_T + 2 + i, tr.at[2, parts[i]], acc_r.at[6, parts[i]], ahead)
 
-    load_lhs(dgut, 0, 2 * F)
-    tiles = cols // TN
-    most = tiles - tiles // 2
-    dw_own(0, 0, most)
-    dx_pairs([cy], k, from_sibling(2), [part.at[2], part.at[3]])
     add([part.at[3], got(UP_OTHER), got(DN_OTHER)], acc_s.at[6])
     for i in range(2):
         send(RS_T + i, acc_s.at[6, parts[i]], tr.at[2, parts[i]], ahead)
-    dw_own(0, most, tiles - most)
+    dw_own(0, few, tiles - few)
     onward(0)
-    dw_own(1, 0, most)
     onward(1)
-    dw_own(1, most, tiles - most)
+    dw_own(1, 0, tiles)
     arrived(R_DWD, dwd_r)
     got(UP_OWN)
     got(DN_OWN)

time: 545 us -> 541 us (level)
  no operation moved by 1% of the time
where the time goes in v3:
time: 541 us; the launch traced here: 537 us
  Pallas kernels  519 us (96%)
  other arithmetic  9.5 us (2%)
  local copies, waits for them, and re-layouts  7.65 us (1%)
    pallas_call x1, Pallas kernels, body(): pl.pallas_call(functools.partial(kernel, side), out_shape=shapes, in_spec...  519 us

profile of v3, /device:TPU:97, one launch (start us, length us, event | category | flops | bytes accessed | tf_op | source)
XLA Modules:
  0.0 537.0 jit_solution(13382365422322951145)
XLA Ops:
  0.6 519.2 %shard_map.102 = (bf16[5120,384]{1,0:T(8,128)(2,1)}, bf16[5120,384]{1,0:T(8,128)(2,1)}, bf16[3584,5120]{1,0:T(8,128)(2,1)}, bf16[3584,5120]{1,0:T(8,128)(2,1)}, ...) custom-call(bf16[224,5120]{1,0:T(8,128)(2,1)} %x.1, ...), custom_call_target="tpu_custom_call" | custom-call | tf_op jit(solution)/shard_map/pallas_call | solution.py:471
  519.8 0.0 copy-start
  519.8 0.0 copy-start.3
  519.8 6.3 %fusion = bf16[224,5120]{1,0:T(8,128)(2,1)} fusion(f32[4,224,5120]{2,1,0:T(8,128)} %get-tuple-element.10, bf16[7,224,5120]{2,1,0:T(8,128)(2,1)} %get-tuple-element.11), kind=kLoop, calls=%fused_computation.2 | loop fusion | flops 8028160 | bytes 13762560 | tf_op jit(solution)/shard_map/add | solution.py:490
  526.2 1.1 copy-done
  527.2 1.1 copy-done.3
  528.3 0.0 copy-start.2
  528.3 3.2 add_convert_fusion
  531.5 0.0 copy-done.2
  531.5 0.0 copy-start.1
  531.5 2.0 copy.13
  533.5 1.5 copy-done.1
  535.1 1.9 copy.14
Async XLA Ops:
  519.8 7.4 %copy-start = (f32[384,5120]{1,0:T(8,128)S(1)}, f32[384,5120]{1,0:T(8,128)}, u32[]{:S(2)}) copy-start(f32[384,5120]{1,0:T(8,128)} %get-tuple-element.14) | copy-start | bytes 23592964
  519.8 8.5 %copy-start.3 = (bf16[384,5120]{1,0:T(8,128)(2,1)S(1)}, bf16[384,5120]{1,0:T(8,128)(2,1)}, u32[]{:S(2)}) copy-start(bf16[384,5120]{1,0:T(8,128)(2,1)} %get-tuple-element.15) | copy-start | bytes 11796484
  528.3 3.2 copy-start.2
  531.5 3.5 copy-start.1
